TPU v7x, 32 devices: a whole 2x2x4 slice. The times are simulated.
32 devices in a mesh: gy: 2 (over core), gx: 16 (over z, y, x).
Axes of the slice: x: 2, y: 2, z: 4, core: 2. Of those that a mesh axis runs over, the one named last changes fastest.
Arguments:
- basis_vectors: float32 [36, 64, 128, 256], P(None, 'gx', 'gy'), may hold values from -30 to 30, as said below
- reaction: float32 [64, 128, 256], P('gx', 'gy'), may hold values from 0.5 to 3
Outputs:
- new_vectors: float32 [4, 64, 128, 256], P(None, 'gx', 'gy')
- hessenberg: float32 [40, 4], replicated
Inputs may be any that keep to these rules, and one draw needn't show every extreme that they name: `basis_vectors`: under the inner product the basis vectors are nearly orthonormal.
All inputs are finite; a program needn't handle non-finite values.
Results may differ from a plain program's by a relative error of at most 0.0003.
Values sent between devices are 32-bit elements; how exact they have to be, the bound alone decides.
A program may use at most 128 MiB of HBM per device.

v0:
```python
import jax
import jax.numpy as jnp
from jax import lax
from jax.sharding import PartitionSpec as P

STEPS = 4
WIND_SPEEDS = (0.9, 0.6, 0.4)
EPSILON = 1e-06


def with_halo(cells, sides, width):
    for axis, dim in sides:
        count = lax.axis_size(axis)
        ends = count - 1
        head = lax.slice_in_dim(cells, 0, width, axis=dim)
        tail = lax.slice_in_dim(cells, cells.shape[dim] - width, cells.shape[dim], axis=dim)
        cells = jnp.concatenate(
            [
                lax.ppermute(tail, axis, [(i, (i + 1) % count) for i in range(ends)]),
                cells,
                lax.ppermute(head, axis, [((i + 1) % count, i) for i in range(ends)]),
            ],
            axis=dim,
        )
    return cells


def stencil(values, x_ext, y_ext, z_ext, reaction):
    summed = -reaction * values
    for position, extended in enumerate((x_ext, y_ext, z_ext)):
        count = values.shape[position]
        higher = lax.slice_in_dim(extended, 3, count + 3, axis=position)
        lower_one = lax.slice_in_dim(extended, 1, count + 1, axis=position)
        lower_two = lax.slice_in_dim(extended, 0, count, axis=position)
        wind_speed = WIND_SPEEDS[position]
        summed = (
            summed
            + higher
            + lower_one
            - 2.0 * values
            - wind_speed * (3.0 * values - 4.0 * lower_one + lower_two) * 0.5
        )
    return summed


def apply_operator(values, reaction):
    rows_x = values.shape[0]
    rows_y = values.shape[1]
    padded = with_halo(values, (("gy", 1), ("gx", 0)), 2)
    x_ext = padded[: rows_x + 3, 2 : rows_y + 2]
    y_ext = padded[2 : rows_x + 2, : rows_y + 3]
    z_ext = jnp.pad(values, ((0, 0), (0, 0), (2, 1)))
    return stencil(values, x_ext, y_ext, z_ext, reaction)


def project(basis_vectors, created, image):
    local = jnp.einsum("kxyz,xyz->k", basis_vectors, image, precision=lax.Precision.HIGHEST)
    extra = [jnp.sum(vector * image)[None] for vector in created]
    return jnp.concatenate([local] + extra)


def combine(basis_vectors, created, weights):
    keep_count = basis_vectors.shape[0]
    summed = jnp.einsum(
        "k,kxyz->xyz", weights[:keep_count], basis_vectors, precision=lax.Precision.HIGHEST
    )
    for index, vector in enumerate(created):
        summed = summed + weights[keep_count + index] * vector
    return summed


def body(basis_vectors, reaction):
    keep_count = basis_vectors.shape[0]
    basis_size = keep_count + STEPS
    cell_count = float(
        basis_vectors.shape[1]
        * basis_vectors.shape[2]
        * basis_vectors.shape[3]
        * lax.axis_size("gx")
        * lax.axis_size("gy")
    )
    created = []
    columns = []
    local_gram = jnp.einsum(
        "axyz,bxyz->ab", basis_vectors, basis_vectors, precision=lax.Precision.HIGHEST
    )
    kept_gram = lax.psum(local_gram, ("gy", "gx")) / cell_count
    gram_matrix = (
        jnp.zeros((basis_size, basis_size), jnp.float32).at[:keep_count, :keep_count].set(kept_gram)
    )
    for section in range(STEPS):
        current = keep_count + section
        vector_now = basis_vectors[keep_count - 1] if section == 0 else created[-1]
        image = apply_operator(vector_now, reaction)
        first_terms = lax.psum(project(basis_vectors, created, image), ("gy", "gx")) / cell_count
        first_rest = image - combine(basis_vectors, created, first_terms)
        second_terms, rest_square = lax.psum(
            (project(basis_vectors, created, first_rest), jnp.sum(first_rest * first_rest)),
            ("gy", "gx"),
        )
        second_terms = second_terms / cell_count
        rest_square = rest_square / cell_count
        gram_now = gram_matrix[:current, :current]
        folded = jnp.dot(gram_now, second_terms, precision=lax.Precision.HIGHEST)
        second_rest = first_rest - combine(basis_vectors, created, second_terms)
        squared = (
            rest_square
            - 2.0 * jnp.sum(second_terms * second_terms)
            + jnp.sum(second_terms * folded)
        )
        length_now = jnp.sqrt(squared + EPSILON)
        cross_terms = (second_terms - folded) / length_now
        gram_matrix = gram_matrix.at[:current, current].set(cross_terms)
        gram_matrix = gram_matrix.at[current, :current].set(cross_terms)
        gram_matrix = gram_matrix.at[current, current].set(squared / (length_now * length_now))
        weights = first_terms + second_terms
        columns.append(
            jnp.concatenate(
                [weights, length_now[None], jnp.zeros((basis_size - current - 1,), jnp.float32)]
            )
        )
        created.append(second_rest / length_now)
    return (jnp.stack(created), jnp.stack(columns, axis=1))


def solution(mesh):
    in_specs = (P(None, "gx", "gy", None), P("gx", "gy", None))
    out_specs = (P(None, "gx", "gy", None), P())
    return jax.shard_map(body, mesh=mesh, in_specs=in_specs, out_specs=out_specs, check_vma=False)
```

profile of v0, /device:TPU:0, one launch (start us, length us, event | category | flops | bytes accessed | tf_op | source)
XLA Modules:
  0.0 709.3 jit_solution(1123148927254146616)
XLA Ops:
  3.4 3.2 collective-permute-start
  6.6 25.4 %fusion.34 = f32[36,36]{1,0:T(8,128)S(1)} fusion(f32[36,4,64,256]{3,2,1,0:T(8,128)} %param.22), kind=kOutput, calls=%fused_computation.34 | convolution fusion | flops 1019215872 | bytes 9442368 | tf_op jit(solution)/shard_map/axyz,bxyz->ab/dot_general | solution.py:84
  34.7 4.7 collective-permute-start.3
  42.1 5.0 collective-permute-done.2
  47.6 13.0 %fusion.38 = f32[36]{0:T(128)S(1)} fusion(f32[36,4,64,256]{3,2,1,0:T(8,128)S(1)} %copy-done, f32[4,64,256,1]{2,1,0,3:T(8,128)S(1)} %bitcast.235), kind=kOutput, calls=%fused_computation.40 | convolution fusion | flops 28311552 | bytes 9699472 | tf_op jit(solution)/shard_map/kxyz,xyz->k/dot_general | solution.py:57
  61.3 42.1 %psum.91 = f32[36]{0:T(128)S(1)} all-reduce(f32[36]{0:T(128)S(1)} %fusion.38), channel_id=1, replica_groups=mesh['gy'=2,'gx'=16] {'gy','gx'}, use_global_device_ids=true, to_apply=%region_0.0 | all-reduce | flops 36 | bytes 288 | tf_op jit(solution)/shard_map/psum | solution.py:95
  103.4 14.5 %fusion.26 = f32[1,4,64,256]{3,0,2,1:T(1,128)S(1)} fusion(f32[36,4,64,256]{3,2,1,0:T(8,128)} %param.22, f32[36]{0:T(128)S(1)} %psum.91), kind=kOutput, calls=%fused_computation.26 | convolution fusion | flops 28311588 | bytes 9699472 | tf_op jit(solution)/shard_map/k,kxyz->xyz/dot_general | solution.py:64
  118.6 15.8 %fusion.41 = f32[36]{0:T(128)S(1)} fusion(f32[36,4,64,256]{3,2,1,0:T(8,128)} %param.22, f32[4,64,256,1]{2,1,0,3:T(8,128)S(1)} %get-tuple-element.159), kind=kOutput, calls=%fused_computation.41 | convolution fusion | flops 28311552 | bytes 9699472 | tf_op jit(solution)/shard_map/kxyz,xyz->k/dot_general | solution.py:57
  134.4 39.9 %all-reduce.8 = (f32[36]{0:T(128)S(1)}, f32[]{:T(128)}, f32[36,36]{1,0:T(8,128)S(1)}) all-reduce(f32[36]{0:T(128)S(1)} %fusion.41, f32[]{:T(128)} %get-tuple-element.158, f32[36,36]{1,0:T(8,128)S(1)} %fusion.34), channel_id=1, replica_groups=mesh['gy'=2,'gx'=16] {'gy','gx'}, use_global_device_ids=true, to_apply=%region_1.0 | all-reduce | flops 1333 | bytes 10664 | tf_op jit(solution)/shard_map/psum | solution.py:97
  175.1 14.5 %fusion.22 = f32[1,4,64,256]{3,0,2,1:T(1,128)S(1)} fusion(f32[36,4,64,256]{3,2,1,0:T(8,128)} %param.22, f32[36]{0:T(128)S(1)} %get-tuple-element.148), kind=kOutput, calls=%fused_computation.22 | convolution fusion | flops 28311588 | bytes 9699472 | tf_op jit(solution)/shard_map/k,kxyz->xyz/dot_general | solution.py:64
  193.0 3.0 collective-permute-start.4
  198.2 4.8 collective-permute-start.7
  203.0 1.9 dynamic-slice_select_fusion.2
  205.0 1.7 scatter.35
  207.0 2.1 collective-permute-done.7
  210.2 16.0 %fusion.44 = f32[36]{0:T(128)S(1)} fusion(f32[36,4,64,256]{3,2,1,0:T(8,128)} %param.22, f32[4,64,256,1]{2,1,0,3:T(8,128)S(1)} %bitcast.241), kind=kOutput, calls=%fused_computation.42 | convolution fusion | flops 28311552 | bytes 9699472 | tf_op jit(solution)/shard_map/kxyz,xyz->k/dot_general | solution.py:57
  226.9 41.7 %psum.95 = f32[37]{0:T(128)S(1)} all-reduce(f32[37]{0:T(128)S(1)} %pad_maximum_fusion.26), channel_id=1, replica_groups=mesh['gy'=2,'gx'=16] {'gy','gx'}, use_global_device_ids=true, to_apply=%region_8.9 | all-reduce | flops 37 | bytes 296 | tf_op jit(solution)/shard_map/psum | solution.py:95
  269.2 14.5 %fusion.18 = f32[1,4,64,256]{3,0,2,1:T(1,128)S(1)} fusion(f32[36,4,64,256]{3,2,1,0:T(8,128)} %param.22, f32[37]{0:T(128)S(1)} %broadcast_multiply_fusion.6), kind=kOutput, calls=%fused_computation.18 | convolution fusion | flops 28311552 | bytes 9699476 | tf_op jit(solution)/shard_map/k,kxyz->xyz/dot_general | solution.py:64
  285.1 16.1 %fusion.47 = f32[36]{0:T(128)S(1)} fusion(f32[36,4,64,256]{3,2,1,0:T(8,128)} %param.22, f32[4,64,256,1]{2,1,0,3:T(8,128)S(1)} %bitcast.236), kind=kOutput, calls=%fused_computation.43 | convolution fusion | flops 28311552 | bytes 9699472 | tf_op jit(solution)/shard_map/kxyz,xyz->k/dot_general | solution.py:57
  301.9 39.9 %all-reduce.7 = (f32[37]{0:T(128)S(1)}, f32[]{:T(128)}) all-reduce(f32[37]{0:T(128)S(1)} %pad_maximum_fusion.27, f32[]{:T(128)} %get-tuple-element.134), channel_id=1, replica_groups=mesh['gy'=2,'gx'=16] {'gy','gx'}, use_global_device_ids=true, to_apply=%region_10.11 | all-reduce | flops 38 | bytes 304 | tf_op jit(solution)/shard_map/psum | solution.py:97
  345.1 14.5 %fusion.14 = f32[1,4,64,256]{3,0,2,1:T(1,128)S(1)} fusion(f32[36,4,64,256]{3,2,1,0:T(8,128)} %param.22, f32[37]{0:T(128)S(1)} %get-tuple-element.197), kind=kOutput, calls=%fused_computation.14 | convolution fusion | flops 28311552 | bytes 9699476 | tf_op jit(solution)/shard_map/k,kxyz->xyz/dot_general | solution.py:64
  361.5 3.0 collective-permute-start.8
  366.7 4.8 collective-permute-start.11
  371.5 1.9 dynamic-slice_select_fusion.1
  373.5 1.7 scatter.40
  375.5 2.7 collective-permute-done.11
  379.4 16.3 %fusion.50 = f32[36]{0:T(128)S(1)} fusion(f32[36,4,64,256]{3,2,1,0:T(8,128)} %param.22, f32[4,64,256,1]{2,1,0,3:T(8,128)S(1)} %bitcast.240), kind=kOutput, calls=%fused_computation.44 | convolution fusion | flops 28311552 | bytes 9699472 | tf_op jit(solution)/shard_map/kxyz,xyz->k/dot_general | solution.py:57
  397.1 41.7 %psum.98 = f32[38]{0:T(128)S(1)} all-reduce(f32[38]{0:T(128)S(1)} %pad_maximum_fusion.28), channel_id=1, replica_groups=mesh['gy'=2,'gx'=16] {'gy','gx'}, use_global_device_ids=true, to_apply=%region_18.19 | all-reduce | flops 38 | bytes 304 | tf_op jit(solution)/shard_map/psum | solution.py:95
  439.5 14.5 %fusion.10 = f32[1,4,64,256]{3,0,2,1:T(1,128)S(1)} fusion(f32[36,4,64,256]{3,2,1,0:T(8,128)} %param.22, f32[38]{0:T(128)S(1)} %broadcast_multiply_fusion.4), kind=kOutput, calls=%fused_computation.10 | convolution fusion | flops 28311552 | bytes 9699480 | tf_op jit(solution)/shard_map/k,kxyz->xyz/dot_general | solution.py:64
  454.0 2.0 multiply_reduce_fusion.7
  456.0 16.0 %fusion.53 = f32[36]{0:T(128)S(1)} fusion(f32[36,4,64,256]{3,2,1,0:T(8,128)} %param.22, f32[4,64,256,1]{2,1,0,3:T(8,128)S(1)} %bitcast.239), kind=kOutput, calls=%fused_computation.45 | convolution fusion | flops 28311552 | bytes 9699472 | tf_op jit(solution)/shard_map/kxyz,xyz->k/dot_general | solution.py:57
  473.3 39.1 %all-reduce.6 = (f32[38]{0:T(128)S(1)}, f32[]{:T(128)}) all-reduce(f32[38]{0:T(128)S(1)} %pad_maximum_fusion.29, f32[]{:T(128)} %get-tuple-element.129), channel_id=1, replica_groups=mesh['gy'=2,'gx'=16] {'gy','gx'}, use_global_device_ids=true, to_apply=%region_21.22 | all-reduce | flops 39 | bytes 312 | tf_op jit(solution)/shard_map/psum | solution.py:97
  515.9 14.5 %fusion.6 = f32[1,4,64,256]{3,0,2,1:T(1,128)S(1)} fusion(f32[36,4,64,256]{3,2,1,0:T(8,128)} %param.22, f32[38]{0:T(128)S(1)} %get-tuple-element.188), kind=kOutput, calls=%fused_computation.6 | convolution fusion | flops 28311552 | bytes 9699480 | tf_op jit(solution)/shard_map/k,kxyz->xyz/dot_general | solution.py:64
  533.0 3.0 collective-permute-start.12
  536.9 4.2 collective-permute-start.15
  541.1 2.0 dynamic-slice_select_fusion
  544.4 1.6 scatter.45
  546.5 4.2 collective-permute-done.14
  551.9 16.3 %fusion.56 = f32[36]{0:T(128)S(1)} fusion(f32[36,4,64,256]{3,2,1,0:T(8,128)} %param.22, f32[4,64,256,1]{2,1,0,3:T(8,128)S(1)} %bitcast.237), kind=kOutput, calls=%fused_computation.46 | convolution fusion | flops 28311552 | bytes 9699472 | tf_op jit(solution)/shard_map/kxyz,xyz->k/dot_general | solution.py:57
  568.1 2.1 pad_maximum_fusion.30
  570.2 41.5 %psum.101 = f32[39]{0:T(128)S(1)} all-reduce(f32[39]{0:T(128)S(1)} %pad_maximum_fusion.30), channel_id=1, replica_groups=mesh['gy'=2,'gx'=16] {'gy','gx'}, use_global_device_ids=true, to_apply=%region_30.31 | all-reduce | flops 39 | bytes 312 | tf_op jit(solution)/shard_map/psum | solution.py:95
  612.3 14.5 %fusion.2 = f32[1,4,64,256]{3,0,2,1:T(1,128)S(1)} fusion(f32[36,4,64,256]{3,2,1,0:T(8,128)} %param.22, f32[39]{0:T(128)S(1)} %broadcast_multiply_fusion.2), kind=kOutput, calls=%fused_computation.2 | convolution fusion | flops 28311552 | bytes 9699484 | tf_op jit(solution)/shard_map/k,kxyz->xyz/dot_general | solution.py:64
  626.8 2.8 multiply_reduce_fusion
  629.6 16.0 %fusion.59 = f32[36]{0:T(128)S(1)} fusion(f32[36,4,64,256]{3,2,1,0:T(8,128)} %param.22, f32[4,64,256,1]{2,1,0,3:T(8,128)S(1)} %bitcast.238), kind=kOutput, calls=%fused_computation.47 | convolution fusion | flops 28311552 | bytes 9699472 | tf_op jit(solution)/shard_map/kxyz,xyz->k/dot_general | solution.py:57
  645.7 2.0 pad_maximum_fusion.31
  647.6 39.2 %all-reduce.5 = (f32[39]{0:T(128)S(1)}, f32[]{:T(128)}) all-reduce(f32[39]{0:T(128)S(1)} %pad_maximum_fusion.31, f32[]{:T(128)} %get-tuple-element.122), channel_id=1, replica_groups=mesh['gy'=2,'gx'=16] {'gy','gx'}, use_global_device_ids=true, to_apply=%region_34.35 | all-reduce | flops 40 | bytes 320 | tf_op jit(solution)/shard_map/psum | solution.py:97
  688.1 14.5 %fusion.28 = f32[1,4,64,256]{3,0,2,1:T(1,128)S(1)} fusion(f32[36,4,64,256]{3,2,1,0:T(8,128)} %param.22, f32[39]{0:T(128)S(1)} %get-tuple-element.181), kind=kOutput, calls=%fused_computation.28 | convolution fusion | flops 28311552 | bytes 9699484 | tf_op jit(solution)/shard_map/k,kxyz->xyz/dot_general | solution.py:64
  706.0 2.0 fusion.135
  (105 shorter events, 41.6 us)
Async XLA Ops:
  0.6 31.3 %copy-start.2 = (s32[2]{0:T(128)S(1)}, s32[2]{0:T(128)}, u32[]{:S(2)}) copy-start(s32[2]{0:T(128)} %constant.309.clone.1) | copy-start | bytes 28
  0.6 32.0 %copy-start.4 = (s32[2]{0:T(128)S(1)}, s32[2]{0:T(128)}, u32[]{:S(2)}) copy-start(s32[2]{0:T(128)} %constant.307.clone.1) | copy-start | bytes 28
  0.7 32.7 %copy-start.3 = (s32[2]{0:T(128)S(1)}, s32[2]{0:T(128)}, u32[]{:S(2)}) copy-start(s32[2]{0:T(128)} %constant.304.clone.1) | copy-start | bytes 28
  0.7 46.9 %copy-start = (f32[36,4,64,256]{3,2,1,0:T(8,128)S(1)}, f32[36,4,64,256]{3,2,1,0:T(8,128)}, u32[]{:S(2)}) copy-start(f32[36,4,64,256]{3,2,1,0:T(8,128)} %param.22) | copy-start | bytes 28311556
  0.7 46.5 %copy-start.1 = (f32[4,64,256]{2,1,0:T(8,128)S(1)}, f32[4,64,256]{2,1,0:T(8,128)}, u32[]{:S(2)}) copy-start(f32[4,64,256]{2,1,0:T(8,128)} %param.23) | copy-start | bytes 786436
  1.8 32.7 %collective-permute-start.1 = (f32[4,2,256]{2,1,0:T(2,128)S(1)}, f32[4,2,256]{2,1,0:T(2,128)S(1)}, u32[]{:S(2)}, u32[]{:S(2)}) collective-permute-start(f32[4,2,256]{2,1,0:T(2,128)S(1)} %get-tuple-element.174), channel_id=1, source_target_pairs={{16,0},{17,1},{18,2},{19,3},{20,4},{21,5},{22,6},{23,7},{24,8},{25... | collective-permute-start | bytes 24584 | tf_op jit(solution)/shard_map/ppermute | solution.py:21
  3.4 31.2 %collective-permute-start = (f32[4,2,256]{2,1,0:T(2,128)S(1)}, f32[4,2,256]{2,1,0:T(2,128)S(1)}, u32[]{:S(2)}, u32[]{:S(2)}) collective-permute-start(f32[4,2,256]{2,1,0:T(2,128)S(1)} %get-tuple-element.175), channel_id=1, source_target_pairs={{0,16},{1,17},{2,18},{3,19},{4,20},{5,21},{6,22},{7,23},{8,24},{9,... | collective-permute-start | bytes 24584 | tf_op jit(solution)/shard_map/ppermute | solution.py:19
  34.7 7.4 %collective-permute-start.3 = (f32[2,68,256]{2,1,0:T(8,128)S(1)}, f32[2,68,256]{2,1,0:T(8,128)S(1)}, u32[]{:S(2)}, u32[]{:S(2)}) collective-permute-start(f32[2,68,256]{2,1,0:T(8,128)S(1)} %get-tuple-element.167), channel_id=1, source_target_pairs={{0,1},{1,2},{2,3},{3,4},{4,5},{5,6},{6,7},{7,8},{8,9},{9,10},{10,1... | collective-permute-start | bytes 417800 | tf_op jit(solution)/shard_map/ppermute | solution.py:19
  40.0 7.1 %collective-permute-start.2 = (f32[2,68,256]{2,1,0:T(8,128)S(1)}, f32[2,68,256]{2,1,0:T(8,128)S(1)}, u32[]{:S(2)}, u32[]{:S(2)}) collective-permute-start(f32[2,68,256]{2,1,0:T(8,128)S(1)} %get-tuple-element.166), channel_id=1, source_target_pairs={{1,0},{2,1},{3,2},{4,3},{5,4},{6,5},{7,6},{8,7},{9,8},{10,9},{11,1... | collective-permute-start | bytes 417800 | tf_op jit(solution)/shard_map/ppermute | solution.py:21
  191.7 4.5 collective-permute-start.5
  193.0 3.8 collective-permute-start.4
  196.9 12.3 %collective-permute-start.6 = (f32[2,68,256]{2,1,0:T(8,128)S(1)}, f32[2,68,256]{2,1,0:T(8,128)S(1)}, u32[]{:S(2)}, u32[]{:S(2)}) collective-permute-start(f32[2,68,256]{2,1,0:T(8,128)S(1)} %get-tuple-element.164), channel_id=1, source_target_pairs={{1,0},{2,1},{3,2},{4,3},{5,4},{6,5},{7,6},{8,7},{9,8},{10,9},{11,1... | collective-permute-start | bytes 417800 | tf_op jit(solution)/shard_map/ppermute | solution.py:21
  198.2 10.9 %collective-permute-start.7 = (f32[2,68,256]{2,1,0:T(8,128)S(1)}, f32[2,68,256]{2,1,0:T(8,128)S(1)}, u32[]{:S(2)}, u32[]{:S(2)}) collective-permute-start(f32[2,68,256]{2,1,0:T(8,128)S(1)} %get-tuple-element.165), channel_id=1, source_target_pairs={{0,1},{1,2},{2,3},{3,4},{4,5},{5,6},{6,7},{7,8},{8,9},{9,10},{10,1... | collective-permute-start | bytes 417800 | tf_op jit(solution)/shard_map/ppermute | solution.py:19
  360.2 4.5 collective-permute-start.9
  361.5 3.8 collective-permute-start.8
  365.4 12.9 %collective-permute-start.10 = (f32[2,68,256]{2,1,0:T(8,128)S(1)}, f32[2,68,256]{2,1,0:T(8,128)S(1)}, u32[]{:S(2)}, u32[]{:S(2)}) collective-permute-start(f32[2,68,256]{2,1,0:T(8,128)S(1)} %get-tuple-element.162), channel_id=1, source_target_pairs={{1,0},{2,1},{3,2},{4,3},{5,4},{6,5},{7,6},{8,7},{9,8},{10,9},{11,1... | collective-permute-start | bytes 417800 | tf_op jit(solution)/shard_map/ppermute | solution.py:21
  366.7 11.6 %collective-permute-start.11 = (f32[2,68,256]{2,1,0:T(8,128)S(1)}, f32[2,68,256]{2,1,0:T(8,128)S(1)}, u32[]{:S(2)}, u32[]{:S(2)}) collective-permute-start(f32[2,68,256]{2,1,0:T(8,128)S(1)} %get-tuple-element.163), channel_id=1, source_target_pairs={{0,1},{1,2},{2,3},{3,4},{4,5},{5,6},{6,7},{7,8},{8,9},{9,10},{10,1... | collective-permute-start | bytes 417800 | tf_op jit(solution)/shard_map/ppermute | solution.py:19
  531.7 4.5 collective-permute-start.13
  533.0 3.8 collective-permute-start.12
  536.9 9.6 %collective-permute-start.15 = (f32[2,68,256]{2,1,0:T(8,128)S(1)}, f32[2,68,256]{2,1,0:T(8,128)S(1)}, u32[]{:S(2)}, u32[]{:S(2)}) collective-permute-start(f32[2,68,256]{2,1,0:T(8,128)S(1)} %get-tuple-element.161), channel_id=1, source_target_pairs={{0,1},{1,2},{2,3},{3,4},{4,5},{5,6},{6,7},{7,8},{8,9},{9,10},{10,1... | collective-permute-start | bytes 417800 | tf_op jit(solution)/shard_map/ppermute | solution.py:19
  543.0 7.7 %collective-permute-start.14 = (f32[2,68,256]{2,1,0:T(8,128)S(1)}, f32[2,68,256]{2,1,0:T(8,128)S(1)}, u32[]{:S(2)}, u32[]{:S(2)}) collective-permute-start(f32[2,68,256]{2,1,0:T(8,128)S(1)} %get-tuple-element.160), channel_id=1, source_target_pairs={{1,0},{2,1},{3,2},{4,3},{5,4},{6,5},{7,6},{8,7},{9,8},{10,9},{11,1... | collective-permute-start | bytes 417800 | tf_op jit(solution)/shard_map/ppermute | solution.py:21
where the time goes:
time: 720 us; the launch traced here: 709 us
  blocking collectives  325 us (45%)
  matrix products  270 us (38%)
  starting transfers between devices  41.6 us (6%)
  other arithmetic  33.5 us (5%)
  waiting for transfers between devices  16.6 us (2%)
  local copies, waits for them, and re-layouts  13.3 us (2%)
  between operations  9.55 us (1%)
    psum x4, blocking collectives, body(): lax.psum(project(basis_vectors, created, image), ('gy', 'gx')) / cell_count  167 us
    psum x4, blocking collectives, body(): lax.psum((project(basis_vectors, created, first_rest), jnp.sum(first_rest...  158 us
    dot_general x8, matrix products, project(): jnp.einsum('kxyz,xyz->k', basis_vectors, image, precision=lax.Precision.H...  126 us
    dot_general x8, matrix products, combine(): jnp.einsum('k,kxyz->xyz', weights[:keep_count], basis_vectors, precision=...  116 us
    ppermute x8, starting transfers between devices, with_halo(): lax.ppermute(tail, axis, [(i, (i + 1) % count) for i in range(ends)])  30.8 us
    dot_general x1, matrix products, body(): jnp.einsum('axyz,bxyz->ab', basis_vectors, basis_vectors, precision=lax.P...  25.4 us
  transfers between devices with their start and end apart: 16, of which 8 were waited for; matrix products, arithmetic and copies ran while one was open for 6% of the time, Pallas kernels for 0%

commit v1 on v0

--- a/solution.py
+++ b/solution.py
@@ -92,7 +92,10 @@
         current = keep_count + section
         vector_now = basis_vectors[keep_count - 1] if section == 0 else created[-1]
         image = apply_operator(vector_now, reaction)
-        first_terms = lax.psum(project(basis_vectors, created, image), ("gy", "gx")) / cell_count
+        first_terms = (
+            jnp.sum(lax.all_gather(project(basis_vectors, created, image), ("gy", "gx")), axis=0)
+            / cell_count
+        )
         first_rest = image - combine(basis_vectors, created, first_terms)
         second_terms, rest_square = lax.psum(
             (project(basis_vectors, created, first_rest), jnp.sum(first_rest * first_rest)),

time: 720 us -> 724 us (level)
    unnamed x0 -> x4, blocking collectives: none -> 168 us
    psum x4 -> x0, blocking collectives: 167 us -> none  [body(): lax.psum(project(basis_vectors, created, image), ('gy', 'gx')) / cell_count]
where the time goes in v1:
time: 724 us; the launch traced here: 713 us
  blocking collectives  326 us (45%)
  matrix products  272 us (38%)
  starting transfers between devices  41.4 us (6%)
  other arithmetic  33.9 us (5%)
  waiting for transfers between devices  16.5 us (2%)
  local copies, waits for them, and re-layouts  13.8 us (2%)
  between operations  9.51 us (1%)
    unnamed x4, blocking collectives  168 us
    psum x4, blocking collectives, body(): lax.psum((project(basis_vectors, created, first_rest), jnp.sum(first_rest...  158 us
    dot_general x8, matrix products, project(): jnp.einsum('kxyz,xyz->k', basis_vectors, image, precision=lax.Precision.H...  128 us
    dot_general x8, matrix products, combine(): jnp.einsum('k,kxyz->xyz', weights[:keep_count], basis_vectors, precision=...  116 us
    ppermute x8, starting transfers between devices, with_halo(): lax.ppermute(tail, axis, [(i, (i + 1) % count) for i in range(ends)])  30.8 us
    dot_general x1, matrix products, body(): jnp.einsum('axyz,bxyz->ab', basis_vectors, basis_vectors, precision=lax.P...  25.4 us
  transfers between devices with their start and end apart: 16, of which 8 were waited for; matrix products, arithmetic and copies ran while one was open for 6% of the time, Pallas kernels for 0%

profile of v1, /device:TPU:0, one launch (start us, length us, event | category | flops | bytes accessed | tf_op | source)
XLA Modules:
  0.0 713.0 jit_solution(128027798658046270)
XLA Ops:
  3.0 3.0 collective-permute-start
  6.1 25.4 %fusion.34 = f32[36,36]{1,0:T(8,128)S(1)} fusion(f32[36,4,64,256]{3,2,1,0:T(8,128)} %param.22), kind=kOutput, calls=%fused_computation.34 | convolution fusion | flops 1019215872 | bytes 9442368 | tf_op jit(solution)/shard_map/axyz,bxyz->ab/dot_general | solution.py:84
  34.8 4.9 collective-permute-start.3
  42.3 5.0 collective-permute-done.2
  47.8 15.8 %fusion.38 = f32[36]{0:T(128)S(1)} fusion(f32[36,4,64,256]{3,2,1,0:T(8,128)} %param.22, f32[4,64,256,1]{2,1,0,3:T(8,128)S(1)} %bitcast.235), kind=kOutput, calls=%fused_computation.40 | convolution fusion | flops 28311552 | bytes 9699472 | tf_op jit(solution)/shard_map/kxyz,xyz->k/dot_general | solution.py:57
  63.9 42.2 %all-reduce.5 = f32[1152]{0:T(1024)S(1)} all-reduce(f32[1152]{0:T(1024)S(1)} %dynamic-update-slice.20), channel_id=2, replica_groups=mesh['gy'=2,'gx'=16] {'gy','gx'}, use_global_device_ids=true, to_apply=%add.5 | all-reduce | flops 1152 | bytes 9216
  106.2 14.5 %fusion.26 = f32[1,4,64,256]{3,0,2,1:T(1,128)S(1)} fusion(f32[36,4,64,256]{3,2,1,0:T(8,128)} %param.22, f32[36]{0:T(128)S(1)} %reduce_sum.252), kind=kOutput, calls=%fused_computation.26 | convolution fusion | flops 28311588 | bytes 9699472 | tf_op jit(solution)/shard_map/k,kxyz->xyz/dot_general | solution.py:64
  121.3 16.0 %fusion.41 = f32[36]{0:T(128)S(1)} fusion(f32[36,4,64,256]{3,2,1,0:T(8,128)} %param.22, f32[4,64,256,1]{2,1,0,3:T(8,128)S(1)} %get-tuple-element.159), kind=kOutput, calls=%fused_computation.41 | convolution fusion | flops 28311552 | bytes 9699472 | tf_op jit(solution)/shard_map/kxyz,xyz->k/dot_general | solution.py:57
  137.3 39.7 %all-reduce.12 = (f32[36]{0:T(128)S(1)}, f32[]{:T(128)}, f32[36,36]{1,0:T(8,128)S(1)}) all-reduce(f32[36]{0:T(128)S(1)} %fusion.41, f32[]{:T(128)} %get-tuple-element.158, f32[36,36]{1,0:T(8,128)S(1)} %fusion.34), channel_id=1, replica_groups=mesh['gy'=2,'gx'=16] {'gy','gx'}, use_global_device_ids=true, to_apply=%region_1.0 | all-reduce | flops 1333 | bytes 10664 | tf_op jit(solution)/shard_map/psum | solution.py:100
  177.8 14.5 %fusion.22 = f32[1,4,64,256]{3,0,2,1:T(1,128)S(1)} fusion(f32[36,4,64,256]{3,2,1,0:T(8,128)} %param.22, f32[36]{0:T(128)S(1)} %get-tuple-element.148), kind=kOutput, calls=%fused_computation.22 | convolution fusion | flops 28311588 | bytes 9699472 | tf_op jit(solution)/shard_map/k,kxyz->xyz/dot_general | solution.py:64
  195.7 3.0 collective-permute-start.4
  200.9 4.8 collective-permute-start.7
  205.8 1.9 dynamic-slice_select_fusion.2
  207.7 1.7 scatter.35
  209.7 2.1 collective-permute-done.7
  213.0 16.1 %fusion.44 = f32[36]{0:T(128)S(1)} fusion(f32[36,4,64,256]{3,2,1,0:T(8,128)} %param.22, f32[4,64,256,1]{2,1,0,3:T(8,128)S(1)} %bitcast.241), kind=kOutput, calls=%fused_computation.42 | convolution fusion | flops 28311552 | bytes 9699472 | tf_op jit(solution)/shard_map/kxyz,xyz->k/dot_general | solution.py:57
  229.9 41.9 %all-reduce.6 = f32[1184]{0:T(1024)S(1)} all-reduce(f32[1184]{0:T(1024)S(1)} %maximum_dynamic-update-slice_fusion), channel_id=3, replica_groups=mesh['gy'=2,'gx'=16] {'gy','gx'}, use_global_device_ids=true, to_apply=%add.6 | all-reduce | flops 1184 | bytes 9472
  272.5 14.5 %fusion.18 = f32[1,4,64,256]{3,0,2,1:T(1,128)S(1)} fusion(f32[36,4,64,256]{3,2,1,0:T(8,128)} %param.22, f32[37]{0:T(128)S(1)} %broadcast_multiply_fusion.6), kind=kOutput, calls=%fused_computation.18 | convolution fusion | flops 28311552 | bytes 9699476 | tf_op jit(solution)/shard_map/k,kxyz->xyz/dot_general | solution.py:64
  288.4 16.0 %fusion.47 = f32[36]{0:T(128)S(1)} fusion(f32[36,4,64,256]{3,2,1,0:T(8,128)} %param.22, f32[4,64,256,1]{2,1,0,3:T(8,128)S(1)} %bitcast.236), kind=kOutput, calls=%fused_computation.43 | convolution fusion | flops 28311552 | bytes 9699472 | tf_op jit(solution)/shard_map/kxyz,xyz->k/dot_general | solution.py:57
  305.2 39.8 %all-reduce.11 = (f32[37]{0:T(128)S(1)}, f32[]{:T(128)}) all-reduce(f32[37]{0:T(128)S(1)} %pad_maximum_fusion.26, f32[]{:T(128)} %get-tuple-element.134), channel_id=1, replica_groups=mesh['gy'=2,'gx'=16] {'gy','gx'}, use_global_device_ids=true, to_apply=%region_10.11 | all-reduce | flops 38 | bytes 304 | tf_op jit(solution)/shard_map/psum | solution.py:100
  348.3 14.5 %fusion.14 = f32[1,4,64,256]{3,0,2,1:T(1,128)S(1)} fusion(f32[36,4,64,256]{3,2,1,0:T(8,128)} %param.22, f32[37]{0:T(128)S(1)} %get-tuple-element.197), kind=kOutput, calls=%fused_computation.14 | convolution fusion | flops 28311552 | bytes 9699476 | tf_op jit(solution)/shard_map/k,kxyz->xyz/dot_general | solution.py:64
  364.7 3.0 collective-permute-start.8
  369.9 4.8 collective-permute-start.11
  374.7 1.9 dynamic-slice_select_fusion.1
  376.7 1.7 scatter.40
  378.8 2.7 collective-permute-done.11
  382.7 16.1 %fusion.50 = f32[36]{0:T(128)S(1)} fusion(f32[36,4,64,256]{3,2,1,0:T(8,128)} %param.22, f32[4,64,256,1]{2,1,0,3:T(8,128)S(1)} %bitcast.240), kind=kOutput, calls=%fused_computation.44 | convolution fusion | flops 28311552 | bytes 9699472 | tf_op jit(solution)/shard_map/kxyz,xyz->k/dot_general | solution.py:57
  400.2 42.1 %all-reduce.7 = f32[1216]{0:T(1024)S(1)} all-reduce(f32[1216]{0:T(1024)S(1)} %maximum_dynamic-update-slice_fusion.1), channel_id=4, replica_groups=mesh['gy'=2,'gx'=16] {'gy','gx'}, use_global_device_ids=true, to_apply=%add.7 | all-reduce | flops 1216 | bytes 9728
  443.1 14.5 %fusion.10 = f32[1,4,64,256]{3,0,2,1:T(1,128)S(1)} fusion(f32[36,4,64,256]{3,2,1,0:T(8,128)} %param.22, f32[38]{0:T(128)S(1)} %broadcast_multiply_fusion.4), kind=kOutput, calls=%fused_computation.10 | convolution fusion | flops 28311552 | bytes 9699480 | tf_op jit(solution)/shard_map/k,kxyz->xyz/dot_general | solution.py:64
  457.5 2.0 multiply_reduce_fusion.7
  459.5 16.0 %fusion.53 = f32[36]{0:T(128)S(1)} fusion(f32[36,4,64,256]{3,2,1,0:T(8,128)} %param.22, f32[4,64,256,1]{2,1,0,3:T(8,128)S(1)} %bitcast.239), kind=kOutput, calls=%fused_computation.45 | convolution fusion | flops 28311552 | bytes 9699472 | tf_op jit(solution)/shard_map/kxyz,xyz->k/dot_general | solution.py:57
  476.8 39.0 %all-reduce.10 = (f32[38]{0:T(128)S(1)}, f32[]{:T(128)}) all-reduce(f32[38]{0:T(128)S(1)} %pad_maximum_fusion.27, f32[]{:T(128)} %get-tuple-element.129), channel_id=1, replica_groups=mesh['gy'=2,'gx'=16] {'gy','gx'}, use_global_device_ids=true, to_apply=%region_21.22 | all-reduce | flops 39 | bytes 312 | tf_op jit(solution)/shard_map/psum | solution.py:100
  519.3 14.5 %fusion.6 = f32[1,4,64,256]{3,0,2,1:T(1,128)S(1)} fusion(f32[36,4,64,256]{3,2,1,0:T(8,128)} %param.22, f32[38]{0:T(128)S(1)} %get-tuple-element.188), kind=kOutput, calls=%fused_computation.6 | convolution fusion | flops 28311552 | bytes 9699480 | tf_op jit(solution)/shard_map/k,kxyz->xyz/dot_general | solution.py:64
  536.4 3.0 collective-permute-start.12
  540.3 4.2 collective-permute-start.15
  544.5 2.0 dynamic-slice_select_fusion
  547.9 1.6 scatter.45
  549.9 4.2 collective-permute-done.14
  555.3 16.1 %fusion.56 = f32[36]{0:T(128)S(1)} fusion(f32[36,4,64,256]{3,2,1,0:T(8,128)} %param.22, f32[4,64,256,1]{2,1,0,3:T(8,128)S(1)} %bitcast.237), kind=kOutput, calls=%fused_computation.46 | convolution fusion | flops 28311552 | bytes 9699472 | tf_op jit(solution)/shard_map/kxyz,xyz->k/dot_general | solution.py:57
  571.4 2.2 maximum_dynamic-update-slice_fusion.2
  573.6 41.8 %all-reduce.8 = f32[1248]{0:T(1024)S(1)} all-reduce(f32[1248]{0:T(1024)S(1)} %maximum_dynamic-update-slice_fusion.2), channel_id=5, replica_groups=mesh['gy'=2,'gx'=16] {'gy','gx'}, use_global_device_ids=true, to_apply=%add.8 | all-reduce | flops 1248 | bytes 9984
  616.2 14.5 %fusion.2 = f32[1,4,64,256]{3,0,2,1:T(1,128)S(1)} fusion(f32[36,4,64,256]{3,2,1,0:T(8,128)} %param.22, f32[39]{0:T(128)S(1)} %broadcast_multiply_fusion.2), kind=kOutput, calls=%fused_computation.2 | convolution fusion | flops 28311552 | bytes 9699484 | tf_op jit(solution)/shard_map/k,kxyz->xyz/dot_general | solution.py:64
  630.6 2.8 multiply_reduce_fusion
  633.5 16.0 %fusion.59 = f32[36]{0:T(128)S(1)} fusion(f32[36,4,64,256]{3,2,1,0:T(8,128)} %param.22, f32[4,64,256,1]{2,1,0,3:T(8,128)S(1)} %bitcast.238), kind=kOutput, calls=%fused_computation.47 | convolution fusion | flops 28311552 | bytes 9699472 | tf_op jit(solution)/shard_map/kxyz,xyz->k/dot_general | solution.py:57
  649.4 2.0 pad_maximum_fusion.28
  651.4 39.2 %all-reduce.9 = (f32[39]{0:T(128)S(1)}, f32[]{:T(128)}) all-reduce(f32[39]{0:T(128)S(1)} %pad_maximum_fusion.28, f32[]{:T(128)} %get-tuple-element.122), channel_id=1, replica_groups=mesh['gy'=2,'gx'=16] {'gy','gx'}, use_global_device_ids=true, to_apply=%region_34.35 | all-reduce | flops 40 | bytes 320 | tf_op jit(solution)/shard_map/psum | solution.py:100
  691.9 14.5 %fusion.28 = f32[1,4,64,256]{3,0,2,1:T(1,128)S(1)} fusion(f32[36,4,64,256]{3,2,1,0:T(8,128)} %param.22, f32[39]{0:T(128)S(1)} %get-tuple-element.181), kind=kOutput, calls=%fused_computation.28 | convolution fusion | flops 28311552 | bytes 9699484 | tf_op jit(solution)/shard_map/k,kxyz->xyz/dot_general | solution.py:64
  709.8 2.0 fusion.135
  (116 shorter events, 42.1 us)
Async XLA Ops:
  0.6 30.8 %copy-start.1 = (s32[2]{0:T(128)S(1)}, s32[2]{0:T(128)}, u32[]{:S(2)}) copy-start(s32[2]{0:T(128)} %constant.309.clone.1) | copy-start | bytes 28
  0.6 31.5 %copy-start.3 = (s32[2]{0:T(128)S(1)}, s32[2]{0:T(128)}, u32[]{:S(2)}) copy-start(s32[2]{0:T(128)} %constant.307.clone.1) | copy-start | bytes 28
  0.7 32.2 %copy-start.2 = (s32[2]{0:T(128)S(1)}, s32[2]{0:T(128)}, u32[]{:S(2)}) copy-start(s32[2]{0:T(128)} %constant.304.clone.1) | copy-start | bytes 28
  0.7 46.7 %copy-start = (f32[4,64,256]{2,1,0:T(8,128)S(1)}, f32[4,64,256]{2,1,0:T(8,128)}, u32[]{:S(2)}) copy-start(f32[4,64,256]{2,1,0:T(8,128)} %param.23) | copy-start | bytes 786436
  1.7 33.0 %collective-permute-start.1 = (f32[4,2,256]{2,1,0:T(2,128)S(1)}, f32[4,2,256]{2,1,0:T(2,128)S(1)}, u32[]{:S(2)}, u32[]{:S(2)}) collective-permute-start(f32[4,2,256]{2,1,0:T(2,128)S(1)} %get-tuple-element.174), channel_id=1, source_target_pairs={{16,0},{17,1},{18,2},{19,3},{20,4},{21,5},{22,6},{23,7},{24,8},{25... | collective-permute-start | bytes 24584 | tf_op jit(solution)/shard_map/ppermute | solution.py:21
  3.0 31.7 %collective-permute-start = (f32[4,2,256]{2,1,0:T(2,128)S(1)}, f32[4,2,256]{2,1,0:T(2,128)S(1)}, u32[]{:S(2)}, u32[]{:S(2)}) collective-permute-start(f32[4,2,256]{2,1,0:T(2,128)S(1)} %get-tuple-element.175), channel_id=1, source_target_pairs={{0,16},{1,17},{2,18},{3,19},{4,20},{5,21},{6,22},{7,23},{8,24},{9,... | collective-permute-start | bytes 24584 | tf_op jit(solution)/shard_map/ppermute | solution.py:19
  34.8 7.5 %collective-permute-start.3 = (f32[2,68,256]{2,1,0:T(8,128)S(1)}, f32[2,68,256]{2,1,0:T(8,128)S(1)}, u32[]{:S(2)}, u32[]{:S(2)}) collective-permute-start(f32[2,68,256]{2,1,0:T(8,128)S(1)} %get-tuple-element.167), channel_id=1, source_target_pairs={{0,1},{1,2},{2,3},{3,4},{4,5},{5,6},{6,7},{7,8},{8,9},{9,10},{10,1... | collective-permute-start | bytes 417800 | tf_op jit(solution)/shard_map/ppermute | solution.py:19
  39.7 7.7 %collective-permute-start.2 = (f32[2,68,256]{2,1,0:T(8,128)S(1)}, f32[2,68,256]{2,1,0:T(8,128)S(1)}, u32[]{:S(2)}, u32[]{:S(2)}) collective-permute-start(f32[2,68,256]{2,1,0:T(8,128)S(1)} %get-tuple-element.166), channel_id=1, source_target_pairs={{1,0},{2,1},{3,2},{4,3},{5,4},{6,5},{7,6},{8,7},{9,8},{10,9},{11,1... | collective-permute-start | bytes 417800 | tf_op jit(solution)/shard_map/ppermute | solution.py:21
  194.4 4.5 collective-permute-start.5
  195.7 3.8 collective-permute-start.4
  199.6 12.3 %collective-permute-start.6 = (f32[2,68,256]{2,1,0:T(8,128)S(1)}, f32[2,68,256]{2,1,0:T(8,128)S(1)}, u32[]{:S(2)}, u32[]{:S(2)}) collective-permute-start(f32[2,68,256]{2,1,0:T(8,128)S(1)} %get-tuple-element.164), channel_id=1, source_target_pairs={{1,0},{2,1},{3,2},{4,3},{5,4},{6,5},{7,6},{8,7},{9,8},{10,9},{11,1... | collective-permute-start | bytes 417800 | tf_op jit(solution)/shard_map/ppermute | solution.py:21
  200.9 10.9 %collective-permute-start.7 = (f32[2,68,256]{2,1,0:T(8,128)S(1)}, f32[2,68,256]{2,1,0:T(8,128)S(1)}, u32[]{:S(2)}, u32[]{:S(2)}) collective-permute-start(f32[2,68,256]{2,1,0:T(8,128)S(1)} %get-tuple-element.165), channel_id=1, source_target_pairs={{0,1},{1,2},{2,3},{3,4},{4,5},{5,6},{6,7},{7,8},{8,9},{9,10},{10,1... | collective-permute-start | bytes 417800 | tf_op jit(solution)/shard_map/ppermute | solution.py:19
  363.4 4.5 collective-permute-start.9
  364.7 3.8 collective-permute-start.8
  368.6 12.9 %collective-permute-start.10 = (f32[2,68,256]{2,1,0:T(8,128)S(1)}, f32[2,68,256]{2,1,0:T(8,128)S(1)}, u32[]{:S(2)}, u32[]{:S(2)}) collective-permute-start(f32[2,68,256]{2,1,0:T(8,128)S(1)} %get-tuple-element.162), channel_id=1, source_target_pairs={{1,0},{2,1},{3,2},{4,3},{5,4},{6,5},{7,6},{8,7},{9,8},{10,9},{11,1... | collective-permute-start | bytes 417800 | tf_op jit(solution)/shard_map/ppermute | solution.py:21
  369.9 11.6 %collective-permute-start.11 = (f32[2,68,256]{2,1,0:T(8,128)S(1)}, f32[2,68,256]{2,1,0:T(8,128)S(1)}, u32[]{:S(2)}, u32[]{:S(2)}) collective-permute-start(f32[2,68,256]{2,1,0:T(8,128)S(1)} %get-tuple-element.163), channel_id=1, source_target_pairs={{0,1},{1,2},{2,3},{3,4},{4,5},{5,6},{6,7},{7,8},{8,9},{9,10},{10,1... | collective-permute-start | bytes 417800 | tf_op jit(solution)/shard_map/ppermute | solution.py:19
  535.1 4.5 collective-permute-start.13
  536.4 3.8 collective-permute-start.12
  540.3 9.6 %collective-permute-start.15 = (f32[2,68,256]{2,1,0:T(8,128)S(1)}, f32[2,68,256]{2,1,0:T(8,128)S(1)}, u32[]{:S(2)}, u32[]{:S(2)}) collective-permute-start(f32[2,68,256]{2,1,0:T(8,128)S(1)} %get-tuple-element.161), channel_id=1, source_target_pairs={{0,1},{1,2},{2,3},{3,4},{4,5},{5,6},{6,7},{7,8},{8,9},{9,10},{10,1... | collective-permute-start | bytes 417800 | tf_op jit(solution)/shard_map/ppermute | solution.py:19
  546.5 7.7 %collective-permute-start.14 = (f32[2,68,256]{2,1,0:T(8,128)S(1)}, f32[2,68,256]{2,1,0:T(8,128)S(1)}, u32[]{:S(2)}, u32[]{:S(2)}) collective-permute-start(f32[2,68,256]{2,1,0:T(8,128)S(1)} %get-tuple-element.160), channel_id=1, source_target_pairs={{1,0},{2,1},{3,2},{4,3},{5,4},{6,5},{7,6},{8,7},{9,8},{10,9},{11,1... | collective-permute-start | bytes 417800 | tf_op jit(solution)/shard_map/ppermute | solution.py:21
